TPU v7x, 128 devices: a whole 4x4x4 slice. The times are simulated.
128 devices in a mesh: tm: 32 (over z, y, core), freq: 4 (over x).
Axes of the slice: x: 4, y: 4, z: 4, core: 2. Of those that a mesh axis runs over, the one named last changes fastest.
Arguments:
- spectrum: bfloat16 [4096, 262144], P('freq', 'tm'), may hold values from 4 to 160
- templates: float32 [4096, 128], P('freq'), may hold values from 0.02 to 2.1
- activations: float32 [128, 262144], P(None, 'tm'), may hold values from 0.06 to 6
- lengths: int32 [512], P('tm'), may hold values from 1 to 512
Outputs:
- new_activations: float32 [128, 262144], P(None, 'tm')
- new_templates: float32 [4096, 128], P('freq')
Inputs may be any that keep to these rules, and one draw needn't show every extreme that they name: Track j holds frame slots j * 512 to (j + 1) * 512 - 1; its first lengths[j] slots are frames, the rest padding whose spectrum is arbitrary.
All inputs are finite; a program needn't handle non-finite values.
Results may differ from a plain program's by a relative error of at most 0.0003.
Values sent between devices are 32-bit elements; how exact they have to be, the bound alone decides.
A program may use at most 128 MiB of HBM per device.

v0:
```python
import jax
import jax.numpy as jnp
from jax import lax
from jax.sharding import PartitionSpec as P

TRACK_LEN = 512
UPDATES = 2


def sent_to_all(x, axis):
    copies = jnp.broadcast_to(x, (lax.axis_size(axis), *x.shape))
    return lax.all_to_all(copies, axis, split_axis=0, concat_axis=0, tiled=True)


def taken_together(x, axis):
    everything = sent_to_all(x, axis)
    return jnp.sum(everything, axis=0)


def in_blocks(x, dim, count):
    before, after = (x.shape[:dim], x.shape[dim + 1 :])
    return jnp.moveaxis(x.reshape(*before, count, -1, *after), dim, 0)


def summed_on_arrival(x, axis, dim):
    count = lax.axis_size(axis)
    parts = lax.all_to_all(in_blocks(x, dim, count), axis, 0, 0, tiled=True)
    return jnp.sum(parts, axis=0)


def laid_out(parts, dim):
    parts = jnp.moveaxis(parts, 0, dim)
    shape = parts.shape
    return parts.reshape(*shape[:dim], shape[dim] * shape[dim + 1], *shape[dim + 2 :])


def gather_directly(x, axis, dim):
    parts = sent_to_all(x, axis)
    return laid_out(parts, dim)


def refine(current, numerator, weight_gram, alive_mask):
    for repeat_index in range(UPDATES):
        denominator = jnp.dot(weight_gram, current, precision=lax.Precision.HIGHEST)
        denominator = jnp.where(alive_mask[None, :], denominator, 1.0)
        current = jnp.where(alive_mask[None, :], current * numerator / denominator, 0.0)
    return current


def body(spectrum, templates, activations, lengths):
    position = lax.broadcasted_iota(jnp.int32, (lengths.shape[0], TRACK_LEN), 1)
    alive_mask = (position < lengths[:, None]).reshape(-1)
    low_templates = templates.astype(jnp.bfloat16)
    contract_rows = (((0,), (0,)), ((), ()))
    local_numerator = lax.dot_general(
        low_templates, spectrum, contract_rows, preferred_element_type=jnp.float32
    )
    local_gram = lax.dot_general(
        templates, templates, contract_rows, precision=lax.Precision.HIGHEST
    )
    numerator = lax.psum_scatter(local_numerator, "freq", scatter_dimension=1, tiled=True)
    weight_gram = taken_together(local_gram, "freq")
    piece_width = numerator.shape[1]
    offset_start = lax.axis_index("freq") * piece_width
    own_acts = lax.dynamic_slice_in_dim(activations, offset_start, piece_width, 1)
    own_mask = lax.dynamic_slice_in_dim(alive_mask, offset_start, piece_width, 0)
    partial_acts = refine(own_acts, numerator, weight_gram, own_mask)
    current = lax.all_gather(partial_acts, "freq", axis=1, tiled=True)
    low_activations = current.astype(jnp.bfloat16)
    contract_cols = (((1,), (1,)), ((), ()))
    local_frame_gram = lax.dot_general(
        current, current, contract_cols, precision=lax.Precision.HIGHEST
    )
    row_count = templates.shape[0] // lax.axis_size("tm")
    cross = summed_on_arrival(
        lax.dot_general(
            spectrum, low_activations, contract_cols, preferred_element_type=jnp.float32
        ),
        "tm",
        0,
    )
    frame_gram = taken_together(local_frame_gram, "tm")
    own_rows = lax.dynamic_slice_in_dim(templates, lax.axis_index("tm") * row_count, row_count, 0)
    updated = own_rows * cross / jnp.dot(own_rows, frame_gram, precision=lax.Precision.HIGHEST)
    new_templates = gather_directly(updated, "tm", 0)
    return (current, new_templates)


def solution(mesh):
    return jax.shard_map(
        body,
        mesh=mesh,
        in_specs=(P("freq", "tm"), P("freq", None), P(None, "tm"), P("tm")),
        out_specs=(P(None, "tm"), P("freq", None)),
        check_vma=False,
    )
```

profile of v0, /device:TPU:1, one launch (start us, length us, event | category | flops | bytes accessed | tf_op | source)
XLA Modules:
  0.0 217.1 jit_solution(262212535081510091)
XLA Ops:
  7.2 0.0 reduce-scatter.2.cloned.1.call-start
  7.2 10.4 %fusion.10 = f32[128,8192]{1,0:T(8,128)} fusion(bf16[1024,8192]{1,0:T(8,128)(2,1)} %param.4, f32[1024,128]{1,0:T(8,128)} %param.5), kind=kOutput, calls=%fused_computation.11 | convolution fusion | flops 2147614720 | bytes 21495808 | tf_op jit(solution)/shard_map/dot_general | solution.py:55
  17.6 0.0 copy-start
  17.6 0.0 copy-start.1
  17.7 0.0 reduce-scatter.2.cloned.1.call-update
  17.7 1.0 copy-done
  18.7 1.0 fusion.16
  19.7 0.7 broadcast_in_dim.41
  20.4 4.8 %all-to-all-start = ((f32[4,128,128]{2,1,0:T(8,128)}), f32[4,128,128]{2,1,0:T(8,128)S(1)}, u32[]{:S(2)}, u32[]{:S(2)}) async-start(f32[4,128,128]{2,1,0:T(8,128)} %broadcast_in_dim.41), calls=%async_computation.1 | async-start | bytes 524288 | tf_op jit(solution)/shard_map/all_to_all | solution.py:12
  25.3 0.0 all-gather.2.cloned.1.call-start
  25.3 0.0 copy-done.1
  25.3 0.1 fusion.12
  25.4 5.4 %all-to-all-done = f32[4,128,128]{2,1,0:T(8,128)S(1)} async-done(((f32[4,128,128]{2,1,0:T(8,128)}), f32[4,128,128]{2,1,0:T(8,128)S(1)}, u32[]{:S(2)}, u32[]{:S(2)}) %all-to-all-start) | async-done | bytes 262176 | tf_op jit(solution)/shard_map/all_to_all | solution.py:12
  30.8 36.9 %reduce-scatter.2.cloned.1.call-done = f32[128,2048]{1,0:T(8,128)} async-done(((f32[128,8192]{1,0:T(8,128)}), f32[128,2048]{1,0:T(8,128)}) %reduce-scatter.2.cloned.1.call-update) | async-done | bytes 1048592 | tf_op jit(solution)/shard_map/reduce_scatter | solution.py:61
  67.8 0.0 copy-start.2
  67.8 3.1 %fusion.3 = f32[128,2048]{1,0:T(8,128)S(1)} fusion(f32[128,128]{1,0:T(8,128)S(1)} %reduce_sum.27, f32[128,2048]{1,0:T(8,128)} %reduce-scatter.2.cloned.1.call-done, f32[128,8192]{1,0:T(8,128)} %param.6, s32[]{:T(128)S(6)} %select_n.20, pred[2048]{0:T(1024)(128)(4,1)S(1)} %dynamic_slice.9), kind=kOutput, calls=%fused_computation.5 | convolution fusion | flops 403701760 | bytes 4262912 | tf_op jit(solution)/shard_map/dot_general | solution.py:44
  70.8 0.0 copy-done.2
  70.8 2.1 fusion.1
  73.0 0.0 all-gather.2.cloned.1.call-update
  73.0 48.3 %all-gather.2.cloned.1.call-done = f32[128,8192]{1,0:T(8,128)} async-done(((f32[128,2048]{1,0:T(8,128)}), f32[128,8192]{1,0:T(8,128)}) %all-gather.2.cloned.1.call-update) | async-done | bytes 4194320 | tf_op jit(solution)/shard_map/all_gather | solution.py:68
  121.2 12.7 %fusion.6 = f32[1024,128]{0,1:T(8,128)S(1)} fusion(bf16[1024,8192]{1,0:T(8,128)(2,1)} %param.4, f32[128,8192]{1,0:T(8,128)} %all-gather.2.cloned.1.call-done), kind=kOutput, calls=%fused_computation.8 | convolution fusion | flops 2148532224 | bytes 21495808 | tf_op jit(solution)/shard_map/dot_general | solution.py:76
  134.0 1.0 copy.7
  135.0 7.9 %all-to-all-start.1 = ((f32[32,32,128]{2,1,0:T(8,128)}), f32[32,32,128]{2,1,0:T(8,128)S(1)}, u32[]{:S(2)}, u32[]{:S(2)}) async-start(f32[32,32,128]{2,1,0:T(8,128)} %bitcast.1), calls=%async_computation.2 | async-start | bytes 1048576 | tf_op jit(solution)/shard_map/all_to_all | solution.py:27
  142.8 7.0 %fusion.17 = f32[128,128]{1,0:T(8,128)S(1)} fusion(f32[128,8192]{1,0:T(8,128)} %all-gather.2.cloned.1.call-done), kind=kOutput, calls=%fused_computation.19 | convolution fusion | flops 1610612736 | bytes 4259840 | tf_op jit(solution)/shard_map/dot_general | solution.py:71
  149.8 4.5 %all-to-all-done.1 = f32[32,32,128]{2,1,0:T(8,128)S(1)} async-done(((f32[32,32,128]{2,1,0:T(8,128)}), f32[32,32,128]{2,1,0:T(8,128)S(1)}, u32[]{:S(2)}, u32[]{:S(2)}) %all-to-all-start.1) | async-done | bytes 524320 | tf_op jit(solution)/shard_map/all_to_all | solution.py:27
  154.3 1.6 broadcast_in_dim.44
  155.8 4.1 %all-to-all-start.2 = ((f32[32,128,128]{2,1,0:T(8,128)}), f32[32,128,128]{2,1,0:T(8,128)S(1)}, u32[]{:S(2)}, u32[]{:S(2)}) async-start(f32[32,128,128]{2,1,0:T(8,128)} %broadcast_in_dim.44), calls=%async_computation.3 | async-start | bytes 4194304 | tf_op jit(solution)/shard_map/all_to_all | solution.py:12
  159.9 28.2 %all-to-all-done.2 = f32[32,128,128]{2,1,0:T(8,128)S(1)} async-done(((f32[32,128,128]{2,1,0:T(8,128)}), f32[32,128,128]{2,1,0:T(8,128)S(1)}, u32[]{:S(2)}, u32[]{:S(2)}) %all-to-all-start.2) | async-done | bytes 2097184 | tf_op jit(solution)/shard_map/all_to_all | solution.py:12
  188.2 0.1 reduce_sum.29
  188.3 0.2 convolution_divide_fusion
  188.5 0.1 broadcast_in_dim.45
  188.6 16.3 %all_to_all.20 = f32[32,32,128]{2,1,0:T(8,128)S(1)} all-to-all(f32[32,32,128]{2,1,0:T(8,128)S(1)} %broadcast_in_dim.45), channel_id=1, replica_groups=mesh['tm'=32,'freq'=4] {'tm'}, dimensions={0} | all-to-all | bytes 1048576 | tf_op jit(solution)/shard_map/all_to_all | solution.py:12
  204.9 4.6 %copy.11 = f32[128,8192]{1,0:T(8,128)} copy(f32[128,8192]{1,0:T(8,128)} %all-gather.2.cloned.1.call-done) | data formatting | bytes 8388608
  209.5 0.8 copy.12
  (4 shorter events, 0.1 us)
Async XLA Ops:
  7.2 60.6 %reduce-scatter.2.cloned.1.call-start = ((), (), s32[]{:S(2)}) async-start(), calls=%async_computation.5 | async-start | bytes 5242880 | tf_op jit(solution)/shard_map/reduce_scatter | solution.py:61
  17.6 1.0 copy-start
  17.6 7.6 %copy-start.1 = (s32[16]{0:T(128)S(1)}, s32[16]{0:T(128)}, u32[]{:S(2)}) copy-start(s32[16]{0:T(128)} %param.7) | copy-start | bytes 196
  20.4 10.4 %all-to-all-start = ((f32[4,128,128]{2,1,0:T(8,128)}), f32[4,128,128]{2,1,0:T(8,128)S(1)}, u32[]{:S(2)}, u32[]{:S(2)}) async-start(f32[4,128,128]{2,1,0:T(8,128)} %broadcast_in_dim.41), calls=%async_computation.1 | async-start | bytes 524288 | tf_op jit(solution)/shard_map/all_to_all | solution.py:12
  25.3 96.0 %all-gather.2.cloned.1.call-start = ((), (), s32[]{:S(2)}) async-start(), calls=%async_computation.6 | async-start | bytes 5242880 | tf_op jit(solution)/shard_map/all_gather | solution.py:68
  67.8 3.1 %copy-start.2 = (f32[128,2048]{1,0:T(8,128)S(1)}, f32[128,2048]{1,0:T(8,128)}, u32[]{:S(2)}) copy-start(f32[128,2048]{1,0:T(8,128)} %reduce-scatter.2.cloned.1.call-done) | copy-start | bytes 3145732
  135.0 19.3 %all-to-all-start.1 = ((f32[32,32,128]{2,1,0:T(8,128)}), f32[32,32,128]{2,1,0:T(8,128)S(1)}, u32[]{:S(2)}, u32[]{:S(2)}) async-start(f32[32,32,128]{2,1,0:T(8,128)} %bitcast.1), calls=%async_computation.2 | async-start | bytes 1048576 | tf_op jit(solution)/shard_map/all_to_all | solution.py:27
  155.8 32.4 %all-to-all-start.2 = ((f32[32,128,128]{2,1,0:T(8,128)}), f32[32,128,128]{2,1,0:T(8,128)S(1)}, u32[]{:S(2)}, u32[]{:S(2)}) async-start(f32[32,128,128]{2,1,0:T(8,128)} %broadcast_in_dim.44), calls=%async_computation.3 | async-start | bytes 4194304 | tf_op jit(solution)/shard_map/all_to_all | solution.py:12
Sparse Core Ops, SparseCore 0:
  17.8 49.9 reduce-scatter.1
  73.1 48.0 all-gather.1
where the time goes:
time: 218 us; the launch traced here: 217 us
  waiting for transfers between devices  123 us (56%)
  matrix products  36.4 us (17%)
  starting transfers between devices  16.8 us (8%)
  blocking collectives  16.3 us (7%)
  between operations  14.1 us (6%)
  local copies, waits for them, and re-layouts  9.77 us (4%)
    all_gather x1, waiting for transfers between devices, body(): current = lax.all_gather(partial_acts, 'freq', axis=1, tiled=True)  48.3 us
    reduce_scatter x1, waiting for transfers between devices, body(): lax.psum_scatter(local_numerator, 'freq', scatter_dimension=1, tiled=True)  36.9 us
    all_to_all x2, waiting for transfers between devices, sent_to_all(): return lax.all_to_all(copies, axis, split_axis=0, concat_axis=0, tiled=True)  33.7 us
    all_to_all x1, blocking collectives, sent_to_all(): return lax.all_to_all(copies, axis, split_axis=0, concat_axis=0, tiled=True)  16.3 us
    dot_general x1, matrix products, body(): lax.dot_general(spectrum, low_activations, contract_cols, preferred_eleme...  12.7 us
    dot_general x1, matrix products, body(): lax.dot_general(low_templates, spectrum, contract_rows, preferred_element...  10.4 us
    all_to_all x2, starting transfers between devices, sent_to_all(): return lax.all_to_all(copies, axis, split_axis=0, concat_axis=0, tiled=True)  8.9 us
    all_to_all x1, starting transfers between devices, summed_on_arrival(): parts = lax.all_to_all(in_blocks(x, dim, count), axis, 0, 0, tiled=True)  7.87 us
  transfers between devices with their start and end apart: 5, of which 5 were waited for; matrix products, arithmetic and copies ran while one was open for 4% of the time, Pallas kernels for 0%

commit v1 on v0

v1 whole, which is shorter than its diff:
```python
import functools

import jax
import jax.numpy as jnp
from jax import lax
from jax.experimental import pallas as pl
from jax.experimental.pallas import tpu as pltpu
from jax.sharding import PartitionSpec as P

MESH = pl.DeviceIdType.MESH
TRACK_LEN = 512
UPDATES = 2
CHUNKS = 8
SIZES = (2048, 4096, 4608, 5120, 5632, 6144, 7168, 8192)
VMEM_LIMIT = 48 * 1024 * 1024

F32 = jnp.float32
BF16 = jnp.bfloat16
VMEM = pltpu.VMEM


def split(x):
    high = x.astype(BF16)
    low = (x - high.astype(F32)).astype(BF16)
    return high, low


def right_operand(m):
    high, low = split(m)
    top = jnp.concatenate([high, low], axis=1)
    bottom = jnp.concatenate([high, jnp.zeros_like(low)], axis=1)
    return jnp.concatenate([top, bottom], axis=0)


def fine_dot(x, operand):
    high, low = split(x)
    both = jnp.dot(jnp.concatenate([high, low], axis=1), operand, preferred_element_type=F32)
    k = both.shape[1] // 2
    return both[:, :k] + both[:, k:]


def fold_quadrants(m):
    k = m.shape[0] // 2
    return (m[:k, :k] + m[k:, k:]) + (m[:k, k:] + m[k:, :k])


def send(src, dst, send_sem, recv_sem, device):
    return pltpu.make_async_remote_copy(
        src_ref=src, dst_ref=dst, send_sem=send_sem, recv_sem=recv_sem,
        device_id=device, device_id_type=MESH,
    )


def numerator_kernel(
    ntm, nfreq, steps, spec_ref, templates_ref, act_ref, count_ref,
    num_ref, act_out_ref, operand_ref, most_ref,
    low_ref, gram_ref, grams_ref, counts_ref, gram_send, gram_recv, count_send, count_recv,
):
    step = pl.program_id(0)
    t = lax.axis_index("tm")
    r = lax.axis_index("freq")

    @pl.when(step == 0)
    def _():
        barrier = pltpu.get_barrier_semaphore()

        @pl.loop(1, ntm)
        def _(k):
            pl.semaphore_signal(barrier, inc=1, device_id=(lax.rem(t + k, ntm), r), device_id_type=MESH)

        @pl.loop(1, nfreq)
        def _(k):
            pl.semaphore_signal(barrier, inc=1, device_id=(t, lax.rem(r + k, nfreq)), device_id_type=MESH)

        turned = templates_ref[...].T
        high_t, low_t = split(turned)
        low_ref[...] = high_t
        high, low = split(templates_ref[...])
        products = jnp.dot(
            jnp.concatenate([high_t, low_t], axis=0),
            jnp.concatenate([high, low], axis=1),
            preferred_element_type=F32,
        )
        gram_ref[...] = fold_quadrants(products)
        pl.semaphore_wait(barrier, ntm + nfreq - 2)

        @pl.loop(1, ntm)
        def _(k):
            send(count_ref, counts_ref.at[k - 1], count_send, count_recv, (lax.rem(t + k, ntm), r)).start()

        for k in range(1, nfreq):
            send(gram_ref, grams_ref.at[k - 1], gram_send.at[k - 1], gram_recv.at[k - 1], (t, lax.rem(r + k, nfreq))).start()

    num = jnp.dot(low_ref[...], spec_ref[...], preferred_element_type=F32)
    num_ref[...] = num.T.reshape(num_ref.shape)
    act_out_ref[...] = act_ref[...].T.reshape(act_out_ref.shape)

    @pl.when(step == steps - 1)
    def _():
        everyone = send(counts_ref, counts_ref, count_send, count_recv, (lax.rem(t + 1, ntm), r))
        everyone.wait_send()
        everyone.wait_recv()
        most = count_ref[...]
        for k in range(ntm - 1):
            most = jnp.maximum(most, counts_ref[k])
        most_ref[...] = most
        gram = gram_ref[...]
        for k in range(1, nfreq):
            copy = send(gram_ref, grams_ref.at[k - 1], gram_send.at[k - 1], gram_recv.at[k - 1], (t, lax.rem(r + k, nfreq)))
            copy.wait_send()
            copy.wait_recv()
            gram = gram + grams_ref[k - 1]
        operand_ref[...] = right_operand(gram)


def numerator_call(mesh, spectrum, templates, activations, count):
    ntm, nfreq = mesh.shape["tm"], mesh.shape["freq"]
    bins, frames = spectrum.shape
    k = templates.shape[1]
    steps = frames // TRACK_LEN
    whole = lambda *shape: pl.BlockSpec(shape, lambda i: (0,) * len(shape))
    return pl.pallas_call(
        functools.partial(numerator_kernel, ntm, nfreq, steps),
        grid=(steps,),
        out_shape=(
            jax.ShapeDtypeStruct((frames // 8, 8, k), F32),
            jax.ShapeDtypeStruct((frames // 8, 8, k), F32),
            jax.ShapeDtypeStruct((2 * k, 2 * k), BF16),
            jax.ShapeDtypeStruct((8, 128), F32),
        ),
        in_specs=[
            pl.BlockSpec((bins, TRACK_LEN), lambda i: (0, i)),
            whole(bins, k),
            pl.BlockSpec((k, TRACK_LEN), lambda i: (0, i)),
            whole(8, 128),
        ],
        out_specs=(
            pl.BlockSpec((TRACK_LEN // 8, 8, k), lambda i: (i, 0, 0)),
            pl.BlockSpec((TRACK_LEN // 8, 8, k), lambda i: (i, 0, 0)),
            whole(2 * k, 2 * k),
            whole(8, 128),
        ),
        scratch_shapes=[
            VMEM((k, bins), BF16),
            VMEM((k, k), F32),
            VMEM((nfreq - 1, k, k), F32),
            VMEM((ntm - 1, 8, 128), F32),
            pltpu.SemaphoreType.DMA((nfreq - 1,)),
            pltpu.SemaphoreType.DMA((nfreq - 1,)),
            pltpu.SemaphoreType.DMA,
            pltpu.SemaphoreType.DMA,
        ],
        compiler_params=pltpu.CompilerParams(
            collective_id=0, has_side_effects=True, vmem_limit_bytes=VMEM_LIMIT,
            dimension_semantics=("arbitrary",),
        ),
        name="numerator",
    )(spectrum, templates, activations, count)


def refine_kernel(
    size, src_ref, num_ref, act_ref, operand_ref, out_ref,
    comp, own, first, direct, second, send_sem, first_sem, direct_sem, second_sem, near_sem, far_sem,
):
    t = lax.axis_index("tm")
    r = lax.axis_index("freq")
    shard, half = size // 4, size // 8
    cw = half // CHUNKS
    right, left, opposite = lax.rem(r + 1, 4), lax.rem(r + 3, 4), lax.rem(r + 2, 4)
    near = ((t, right), (t, left))

    barrier = pltpu.get_barrier_semaphore()
    for device in near:
        pl.semaphore_signal(barrier, inc=1, device_id=device, device_id_type=MESH)

    def rows(base, h, c):
        return pl.ds(pl.multiple_of(base * shard + h * half + c * cw, 8), cw)

    def part(c):
        return pl.ds(pl.multiple_of(c * cw, 8), cw)

    def gather(base, h, c, table, into, offset):
        start = base * shard + h * half + c * cw
        for i in range(cw // 8):
            source = src_ref[start // 8 + i]
            into[pl.ds(pl.multiple_of(start - offset + 8 * i, 8), 8), :] = table[source]

    def first_copy(way, c):
        return send(comp.at[rows(opposite, way, c)], first.at[way, part(c)], send_sem.at[way], first_sem.at[way, c], near[way])

    def direct_copy(way, c):
        return send(comp.at[rows((right, left)[way], 1 - way, c)], direct.at[way, part(c)], send_sem.at[2 + way], direct_sem.at[way, c], near[way])

    def second_copy(way, c):
        return send(first.at[way, part(c)], second.at[way, part(c)], send_sem.at[4 + way], second_sem.at[way, c], near[way])

    def near_copy(way, h, c):
        return send(out_ref.at[rows(r, h, c)], out_ref.at[rows(r, h, c)], send_sem.at[6 + 2 * way + h], near_sem.at[way, h, c], near[way])

    def near_arrival(way, h, c):
        owner = (left, right)[way]
        return send(out_ref.at[rows(owner, h, c)], out_ref.at[rows(owner, h, c)], send_sem.at[6 + 2 * way + h], near_sem.at[way, h, c], near[way])

    def far_copy(way, c):
        owner = (left, right)[way]
        return send(out_ref.at[rows(owner, way, c)], out_ref.at[rows(owner, way, c)], send_sem.at[10 + way], far_sem.at[way, c], near[way])

    def far_arrival(way, c):
        return send(out_ref.at[rows(opposite, way, c)], out_ref.at[rows(opposite, way, c)], send_sem.at[10 + way], far_sem.at[way, c], near[way])

    for way in range(2):
        gather(opposite, way, 0, num_ref, comp, 0)
    pl.semaphore_wait(barrier, 2)
    for way in range(2):
        first_copy(way, 0).start()

    @pl.loop(1, CHUNKS)
    def _(c):
        for way in range(2):
            gather(opposite, way, c, num_ref, comp, 0)
            first_copy(way, c).start()

    @pl.loop(0, CHUNKS)
    def _(c):
        for way in range(2):
            gather((right, left)[way], 1 - way, c, num_ref, comp, 0)
            direct_copy(way, c).start()

    @pl.loop(0, CHUNKS)
    def _(c):
        for way in range(2):
            gather((right, left)[way], way, c, num_ref, comp, 0)
            gather(r, way, c, num_ref, comp, 0)
            gather(r, way, c, act_ref, own, r * shard)

    @pl.loop(0, CHUNKS)
    def _(c):
        for way in range(2):
            first_copy(way, c).wait_recv()
            first[way, part(c), :] = first[way, part(c), :] + comp[rows((right, left)[way], way, c), :]
            second_copy(way, c).start()

    @pl.loop(0, CHUNKS)
    def _(c):
        for h in range(2):
            second_copy(h, c).wait_recv()
            direct_copy(1 - h, c).wait_recv()
            numerator = comp[rows(r, h, c), :] + second[h, part(c), :] + direct[1 - h, part(c), :]
            current = own[pl.ds(pl.multiple_of(h * half + c * cw, 8), cw), :]
            for _ in range(UPDATES):
                current = current * numerator / fine_dot(current, operand_ref[...])
            out_ref[rows(r, h, c), :] = current
            for way in range(2):
                near_copy(way, h, c).start()

    @pl.loop(0, CHUNKS)
    def _(c):
        for way in range(2):
            near_arrival(way, way, c).wait_recv()
            far_copy(way, c).start()

    @pl.loop(0, CHUNKS)
    def _(c):
        for way in range(2):
            near_arrival(way, 1 - way, c).wait_recv()
            far_arrival(way, c).wait_recv()

    for i in range(12):
        whole = first.at[0]
        send(whole, whole, send_sem.at[i], first_sem.at[0, 0], near[0]).wait_send()


def refine_call(size, index, src, num, act, operand):
    frames, k = num.shape[0] * 8, num.shape[2]
    shard, half = size // 4, size // 8
    whole = pl.BlockSpec(memory_space=VMEM)
    return pl.pallas_call(
        functools.partial(refine_kernel, size),
        out_shape=jax.ShapeDtypeStruct((frames, k), F32),
        in_specs=[pl.BlockSpec(memory_space=pltpu.SMEM), whole, whole, whole],
        out_specs=whole,
        scratch_shapes=[
            VMEM((size, k), F32),
            VMEM((shard, k), F32),
            VMEM((2, half, k), F32),
            VMEM((2, half, k), F32),
            VMEM((2, half, k), F32),
            pltpu.SemaphoreType.DMA((12,)),
            pltpu.SemaphoreType.DMA((2, CHUNKS)),
            pltpu.SemaphoreType.DMA((2, CHUNKS)),
            pltpu.SemaphoreType.DMA((2, CHUNKS)),
            pltpu.SemaphoreType.DMA((2, 2, CHUNKS)),
            pltpu.SemaphoreType.DMA((2, CHUNKS)),
        ],
        compiler_params=pltpu.CompilerParams(
            collective_id=2 + index, has_side_effects=True, vmem_limit_bytes=VMEM_LIMIT,
        ),
        name=f"refine_{size}",
    )(src, num, act, operand)


def cross_kernel(steps, start_ref, length_ref, act_ref, spec_ref, templates_ref, out_ref, cross_ref, denominator_ref, gram_ref):
    step = pl.program_id(0)
    x = act_ref[pl.ds(pl.multiple_of(start_ref[step], 8), TRACK_LEN), :]
    position = lax.broadcasted_iota(jnp.int32, x.shape, 0)
    x = jnp.where(position < length_ref[step], x, 0.0)
    turned = x.T
    out_ref[...] = turned
    high, low = split(x)
    high_t, low_t = split(turned)
    products = jnp.dot(
        jnp.concatenate([high_t, low_t], axis=0),
        jnp.concatenate([high, low], axis=1),
        preferred_element_type=F32,
    )
    cross = jnp.dot(spec_ref[...], high, preferred_element_type=F32)

    @pl.when(step == 0)
    def _():
        gram_ref[...] = products
        cross_ref[...] = cross

    @pl.when(step > 0)
    def _():
        gram_ref[...] += products
        cross_ref[...] += cross

    @pl.when(step == steps - 1)
    def _():
        denominator_ref[...] = fine_dot(templates_ref[...], right_operand(fold_quadrants(gram_ref[...])))


def cross_call(starts, lengths, act, spectrum, templates):
    bins, frames = spectrum.shape
    k = templates.shape[1]
    steps = frames // TRACK_LEN
    whole = lambda *shape: pl.BlockSpec(shape, lambda i, *_: (0,) * len(shape))
    return pl.pallas_call(
        functools.partial(cross_kernel, steps),
        grid_spec=pltpu.PrefetchScalarGridSpec(
            num_scalar_prefetch=2,
            grid=(steps,),
            in_specs=[
                whole(frames, k),
                pl.BlockSpec((bins, TRACK_LEN), lambda i, *_: (0, i)),
                whole(bins, k),
            ],
            out_specs=(
                pl.BlockSpec((k, TRACK_LEN), lambda i, *_: (0, i)),
                whole(bins, k),
                whole(bins, k),
            ),
            scratch_shapes=[VMEM((2 * k, 2 * k), F32)],
        ),
        out_shape=(
            jax.ShapeDtypeStruct((k, frames), F32),
            jax.ShapeDtypeStruct((bins, k), F32),
            jax.ShapeDtypeStruct((bins, k), F32),
        ),
        compiler_params=pltpu.CompilerParams(vmem_limit_bytes=VMEM_LIMIT, dimension_semantics=("arbitrary",)),
        name="cross",
    )(starts, lengths, act, spectrum, templates)


def template_kernel(
    ntm, cross_ref, denominator_ref, templates_ref, out_ref,
    pair, acc, land, pair_send, pair_recv, land_send, land_recv, out_send, out_recv, last_send, last_recv,
):
    t = lax.axis_index("tm")
    r = lax.axis_index("freq")
    places = ntm // 2
    core = lax.rem(t, 2)
    place = t // 2
    partner = (place * 2 + 1 - core, r)
    half = cross_ref.shape[0] // 2
    count = half // places

    def peer(k):
        return lax.rem(place + k, places)

    barrier = pltpu.get_barrier_semaphore()
    pl.semaphore_signal(barrier, inc=1, device_id=partner, device_id_type=MESH)

    @pl.loop(1, places)
    def _(k):
        pl.semaphore_signal(barrier, inc=1, device_id=(peer(k) * 2 + core, r), device_id_type=MESH)

    pl.semaphore_wait(barrier, places)

    mine = pl.ds(pl.multiple_of(core * half, 8), half)
    theirs = pl.ds(pl.multiple_of((1 - core) * half, 8), half)
    copies = [
        send(ref.at[theirs], pair.at[i], pair_send.at[i], pair_recv.at[i], partner)
        for i, ref in enumerate((cross_ref, denominator_ref))
    ]
    for copy in copies:
        copy.start()
    for i, (copy, ref) in enumerate(zip(copies, (cross_ref, denominator_ref))):
        copy.wait_recv()
        acc[i] = ref[mine, :] + pair[i]

    def piece(k):
        rows = pl.ds(pl.multiple_of(peer(k) * count, 8), count)
        return send(acc.at[:, rows], land.at[k - 1], land_send, land_recv, (peer(k) * 2 + core, r))

    @pl.loop(1, places)
    def _(k):
        piece(k).start()

    arrivals = send(land, land, land_send, land_recv, partner)
    arrivals.wait_recv()
    rows = pl.ds(pl.multiple_of(place * count, 8), count)
    total = acc[:, rows, :]
    for k in range(1, places):
        total = total + land[k - 1]
    own = pl.ds(pl.multiple_of(core * half + place * count, 8), count)
    out_ref[own, :] = templates_ref[own, :] * total[0] / total[1]

    @pl.loop(1, places)
    def _(k):
        send(out_ref.at[own], out_ref.at[own], out_send, out_recv, (peer(k) * 2 + core, r)).start()

    others = out_ref.at[pl.ds(0, (places - 1) * count)]
    gathered = send(others, others, out_send, out_recv, partner)
    gathered.wait_recv()
    last = send(out_ref.at[mine], out_ref.at[mine], last_send, last_recv, partner)
    last.start()
    last.wait_recv()
    for copy in (*copies, arrivals, gathered, last):
        copy.wait_send()


def template_call(mesh, cross, denominator, templates):
    ntm = mesh.shape["tm"]
    bins, k = templates.shape
    places = ntm // 2
    half = bins // 2
    whole = pl.BlockSpec(memory_space=VMEM)
    return pl.pallas_call(
        functools.partial(template_kernel, ntm),
        out_shape=jax.ShapeDtypeStruct((bins, k), F32),
        in_specs=[whole] * 3,
        out_specs=whole,
        scratch_shapes=[
            VMEM((2, half, k), F32),
            VMEM((2, half, k), F32),
            VMEM((places - 1, 2, half // places, k), F32),
            pltpu.SemaphoreType.DMA((2,)),
            pltpu.SemaphoreType.DMA((2,)),
            pltpu.SemaphoreType.DMA,
            pltpu.SemaphoreType.DMA,
            pltpu.SemaphoreType.DMA,
            pltpu.SemaphoreType.DMA,
            pltpu.SemaphoreType.DMA,
            pltpu.SemaphoreType.DMA,
        ],
        compiler_params=pltpu.CompilerParams(collective_id=1, has_side_effects=True),
        name="templates",
    )(cross, denominator, templates)


def body(mesh, spectrum, templates, activations, lengths):
    frames = spectrum.shape[1]
    tiles = (lengths + 7) // 8
    ends = jnp.cumsum(tiles)
    starts = ends - tiles
    index = jnp.arange(frames // 8, dtype=jnp.int32)
    gaps = TRACK_LEN // 8 - tiles
    src = index + jnp.sum(jnp.where(index[:, None] >= ends[None, :], gaps[None, :], 0), axis=1)
    src = jnp.minimum(src, frames // 8 - 1).astype(jnp.int32)
    count = jnp.broadcast_to(ends[-1].astype(F32), (8, 128))
    num, act, operand, most = numerator_call(mesh, spectrum, templates, activations, count)
    needed = most[0, 0] * 8.0
    branch = jnp.sum(needed > jnp.array(SIZES[:-1], F32)).astype(jnp.int32)
    branches = [functools.partial(refine_call, size, i) for i, size in enumerate(SIZES)]
    current = lax.switch(branch, branches, src, num, act, operand)
    new_activations, cross, denominator = cross_call(starts * 8, lengths, current, spectrum, templates)
    return new_activations, template_call(mesh, cross, denominator, templates)


def solution(mesh):
    return jax.shard_map(
        functools.partial(body, mesh),
        mesh=mesh,
        in_specs=(P("freq", "tm"), P("freq", None), P(None, "tm"), P("tm")),
        out_specs=(P(None, "tm"), P("freq", None)),
        check_vma=False,
    )
```

time: 218 us -> 137 us (0.63)
  Pallas kernels: 0 us -> 124 us
  waiting for transfers between devices: 123 us -> 0 us
  matrix products: 36.4 us -> 0 us
  starting transfers between devices: 16.8 us -> 0 us
  blocking collectives: 16.3 us -> 0 us
  between operations: 14.1 us -> 2.69 us
    pallas_call x0 -> x4, Pallas kernels: none -> 124 us  [the longest x1 56.3 us: refine_call(): pl.pallas_call(functools.partial(refine_kernel, size), out_shape=jax.Shap...]
    all_gather x1 -> x0, waiting for transfers between devices: 48.3 us -> none  [body(): current = lax.all_gather(partial_acts, 'freq', axis=1, tiled=True)]
    all_to_all x3 -> x0, waiting for transfers between devices: 38.2 us -> none  [the longest x2 33.7 us: sent_to_all(): return lax.all_to_all(copies, axis, split_axis=0, concat_axis=0, tiled=True)]
    reduce_scatter x1 -> x0, waiting for transfers between devices: 36.9 us -> none  [body(): lax.psum_scatter(local_numerator, 'freq', scatter_dimension=1, tiled=True)]
    dot_general x7 -> x0, matrix products: 36.4 us -> none  [the longest x1 12.7 us: body(): lax.dot_general(spectrum, low_activations, contract_cols, preferred_eleme...]
    all_to_all x3 -> x0, starting transfers between devices: 16.8 us -> none  [the longest x2 8.9 us: sent_to_all(): return lax.all_to_all(copies, axis, split_axis=0, concat_axis=0, tiled=True)]
    all_to_all x1 -> x0, blocking collectives: 16.3 us -> none  [sent_to_all(): return lax.all_to_all(copies, axis, split_axis=0, concat_axis=0, tiled=True)]
    broadcast_in_dim x3 -> x1, local copies, waits for them, and re-layouts: 2.33 us -> 0.01 us  [body(): count = jnp.broadcast_to(ends[-1].astype(F32), (8, 128))]
  transfers between devices with their start and end apart: 5 -> 0, of which waited for: 5 -> 0; matrix products, arithmetic and copies ran while one was open for 4% -> 0% of each run, Pallas kernels for 0% -> 0%
where the time goes in v1:
time: 137 us; the launch traced here: 136 us
  Pallas kernels  124 us (91%)
  local copies, waits for them, and re-layouts  7.8 us (6%)
  between operations  2.69 us (2%)
  other arithmetic  1.55 us (1%)
    pallas_call x1, Pallas kernels, refine_call(): pl.pallas_call(functools.partial(refine_kernel, size), out_shape=jax.Shap...  56.3 us
    pallas_call x1, Pallas kernels, numerator_call(): pl.pallas_call(functools.partial(numerator_kernel, ntm, nfreq, steps), gr...  24.9 us
    pallas_call x1, Pallas kernels, template_call(): pl.pallas_call(functools.partial(template_kernel, ntm), out_shape=jax.Sha...  22.8 us
    pallas_call x1, Pallas kernels, cross_call(): pl.pallas_call(functools.partial(cross_kernel, steps), grid_spec=pltpu.Pr...  19.6 us
    unnamed x15, local copies, waits for them, and re-layouts  6.68 us

profile of v1, /device:TPU:1, one launch (start us, length us, event | category | flops | bytes accessed | tf_op | source)
XLA Modules:
  0.0 135.7 jit_solution(10554523962379354735)
XLA Ops:
  0.6 0.7 broadcast_subtract_fusion
  1.3 0.1 copy.9
  1.4 0.5 slice.9
  2.6 0.1 reduce
  2.7 0.1 select_reduce_fusion
  2.8 0.0 copy-start
  2.8 1.0 copy-done
  3.9 0.0 copy-start.2
  3.9 2.2 %copy-done.2 = f32[128,8192]{1,0:T(8,128)S(1)} copy-done((f32[128,8192]{1,0:T(8,128)S(1)}, f32[128,8192]{1,0:T(8,128)}, u32[]{:S(2)}) %copy-start.2) | copy-done | bytes 4194328
  6.1 0.0 copy-start.6
  6.1 24.9 %numerator.1 = (f32[1024,8,128]{2,1,0:T(8,128)}, f32[1024,8,128]{2,1,0:T(8,128)}, bf16[256,256]{1,0:T(8,128)(2,1)S(1)}, f32[8,128]{1,0:T(8,128)S(1)}) custom-call(bf16[1024,8192]{1,0:T(8,128)(2,1)} %spec_ref.3, f32[1024,128]{1,0:T(8,128)S(1)} %copy-done, f32[128,8192]{1,0:T(8,128)S(1)} %copy-done.2, f32[8,128]{1,0:T(8,128)S(1)} %broadcast_in_dim.18.count_ref), custom_call_target="tpu_custom_call" | custom-call | tf_op jit(solution)/shard_map/numerator/pallas_call | solution.py:122
  30.9 0.5 slice.8
  32.1 0.0 copy-done.6
  32.1 0.6 fusion
  33.4 0.0 copy-start.1
  33.4 0.0 copy-start.5
  33.4 56.4 %conditional.1 = (f32[8192,128]{1,0:T(8,128)}) conditional(s32[]{:T(128)} %clamp.3, (s32[1024]{0:T(1024)S(1)}, f32[1024,8,128]{2,1,0:T(8,128)}, f32[1024,8,128]{2,1,0:T(8,128)}, bf16[256,256]{1,0:T(8,128)(2,1)S(1)}) %tuple.32, (s32[1024]{0:T(1024)S(1)}, f32[1024,8,128]{2,1,0:T(8,128)}, f32[1024,8,128]{2,1,0:T(8,128)}, ...), branch_computations={%region_3.4_spmd, %region_4.5_spmd, %region_5.6_spmd, %region_6.7_... | conditional | bytes 8 | solution.py:476
  33.5 56.3 %refine_5632.1 = f32[8192,128]{1,0:T(8,128)} custom-call(s32[1024]{0:T(1024)S(1)} %get-tuple-element.89.src_ref, f32[1024,8,128]{2,1,0:T(8,128)} %get-tuple-element.90.num_ref, f32[1024,8,128]{2,1,0:T(8,128)} %get-tuple-element.91.act_ref, bf16[256,256]{1,0:T(8,128)(2,1)S(1)} %get-tuple-element.92.operand_ref), custom_call_target="tpu_custom_call" | custom-call | tf_op jit(solution)/shard_map/cond/branch_4_fun/refine_5632/pallas_call | solution.py:277
  89.8 0.0 copy-done.1
  89.8 0.0 copy-done.5
  89.8 19.6 %cross.1 = (f32[128,8192]{1,0:T(8,128)}, f32[1024,128]{1,0:T(8,128)S(1)}, f32[1024,128]{1,0:T(8,128)S(1)}) custom-call(s32[16]{0:T(128)S(1)} %subtract_multiply_fusion.start_ref, s32[16]{0:T(128)S(1)} %copy-done.5, f32[8192,128]{1,0:T(8,128)} %get-tuple-element.127.act_ref, bf16[1024,8192]{1,0:T(8,128)(2,1)} %spec_ref.3, f32[1024,128]{1,0:T(8,128)S(1)} %copy-done.1), custom_call_target="tpu_custom_call" | custom-call | tf_op jit(solution)/shard_map/cross/pallas_call | solution.py:338
  109.5 0.0 copy-start.3
  109.5 0.8 copy-done.3
  110.2 0.0 copy-start.4
  110.3 0.8 copy-done.4
  111.0 22.8 %templates.1 = f32[1024,128]{1,0:T(8,128)} custom-call(f32[1024,128]{1,0:T(8,128)} %copy-done.3, f32[1024,128]{1,0:T(8,128)} %copy-done.4, f32[1024,128]{1,0:T(8,128)} %templates_ref.5), custom_call_target="tpu_custom_call" | custom-call | tf_op jit(solution)/shard_map/templates/pallas_call | solution.py:439
  133.8 1.9 %copy.19 = f32[1024,128]{1,0:T(8,128)} copy(f32[1024,128]{1,0:T(8,128)} %templates.1) | data formatting | bytes 1048576
  (4 shorter events, 0.1 us)
Async XLA Ops:
  2.8 1.0 copy-start
  3.9 2.2 %copy-start.2 = (f32[128,8192]{1,0:T(8,128)S(1)}, f32[128,8192]{1,0:T(8,128)}, u32[]{:S(2)}) copy-start(f32[128,8192]{1,0:T(8,128)} %act_ref.1) | copy-start | bytes 12582916
  6.1 26.0 %copy-start.6 = (f32[7]{0:T(128)S(1)}, f32[7]{0:T(128)}, u32[]{:S(2)}) copy-start(f32[7]{0:T(128)} %constant.33.clone) | copy-start | bytes 88
  33.4 56.4 %copy-start.1 = (f32[1024,128]{1,0:T(8,128)S(1)}, f32[1024,128]{1,0:T(8,128)}, u32[]{:S(2)}) copy-start(f32[1024,128]{1,0:T(8,128)} %templates_ref.5) | copy-start | bytes 1572868
  33.4 56.4 %copy-start.5 = (s32[16]{0:T(128)S(1)}, s32[16]{0:T(128)}, u32[]{:S(2)}) copy-start(s32[16]{0:T(128)} %length_ref.1) | copy-start | bytes 196
  109.5 0.8 copy-start.3
  110.2 0.8 copy-start.4
